TPU v7x, 128 devices: a whole 4x4x4 slice. The times are simulated.
128 devices in a mesh: row: 8 (over x, core), col: 16 (over y, z).
Axes of the slice: x: 4, y: 4, z: 4, core: 2. Of those that a mesh axis runs over, the one named last changes fastest.
Arguments:
- points: float32 [16, 32768], P(None, ('row', 'col')), may hold values from -6 to 6
- lengthscale: float32 [16], replicated, may hold values from 2 to 8
- signal: float32 [1], replicated, may hold values from 0.5 to 2
- noise: float32 [1], replicated, may hold values from 0.05 to 0.5
- targets: float32 [32768], P(('row', 'col')), may hold values from -12 to 12
- probe_bits: int32 [31, 32768], P(None, ('row', 'col')), may hold values from 0 to 1
Outputs:
- solution: float32 [32, 32768], P(None, ('row', 'col'))
- residual: float32 [32, 32768], P(None, ('row', 'col'))
All inputs are finite; a program needn't handle non-finite values.
Results may differ from a plain program's by a relative error of at most 0.0013.
Values sent between devices are 32-bit elements; how exact they have to be, the bound alone decides.
A program may use at most 128 MiB of HBM per device.

v0:
```python
import jax
import jax.numpy as jnp
from jax import lax
from jax.sharding import Mesh
from jax.sharding import PartitionSpec as P

ITERS = 3
COL = ("col_0", "col_1")
ROW = ("row_0", "row_1")
ROW_COL = ("row_0", "row_1", "col_0", "col_1")


ROOT_FIVE = 5.0**0.5


def copy_for_each(x, axis):
    length = lax.axis_size(axis)
    return lax.all_to_all(jnp.broadcast_to(x[None], (length, *x.shape)), axis, 0, 0, tiled=True)


def laid_out(tiles, dim):
    tiles = jnp.moveaxis(tiles, 0, dim)
    shape = tiles.shape
    return tiles.reshape(*shape[:dim], shape[dim] * shape[dim + 1], *shape[dim + 2 :])


def collect(x, axis, dim):
    tiles = copy_for_each(x, axis)
    return laid_out(tiles, dim)


def in_blocks(x, dim, length):
    shape = x.shape
    tiles = x.reshape(*shape[:dim], length, shape[dim] // length, *shape[dim + 1 :])
    return jnp.moveaxis(tiles, dim, 0)


def summed_on_arrival(x, axis, dim):
    length = lax.axis_size(axis)
    tiles = lax.all_to_all(in_blocks(x, dim, length), axis, 0, 0, tiled=True)
    return jnp.sum(tiles, axis=0)


def by_axis(x, axes):
    for axis in axes:
        x = lax.psum(x, axis)
    return x


def matern_tile(row_scaled, col_scaled, signal_value):
    row_sq = jnp.sum(row_scaled * row_scaled, axis=0)
    col_sq = jnp.sum(col_scaled * col_scaled, axis=0)
    cross_term = lax.dot_general(
        row_scaled,
        col_scaled,
        (((0,), (0,)), ((), ())),
        precision=lax.Precision.HIGHEST,
        preferred_element_type=jnp.float32,
    )
    dist_sq = jnp.maximum(row_sq[:, None] + col_sq[None, :] - 2.0 * cross_term, 0.0)
    radius = jnp.sqrt(dist_sq)
    return (
        signal_value
        * (1.0 + ROOT_FIVE * radius + 5.0 / 3.0 * dist_sq)
        * jnp.exp(-ROOT_FIVE * radius)
    )


def row_blocks(row_scaled):
    row_total = row_scaled.shape[1]
    block_rows = min(1024, row_total)
    block_count = row_total // block_rows
    return row_scaled.reshape(row_scaled.shape[0], block_count, block_rows).transpose(1, 0, 2)


def build_tile(row_scaled, col_scaled, signal_value):
    row_total = row_scaled.shape[1]
    stacked = row_blocks(row_scaled)

    def one_block(row_block):
        return matern_tile(row_block, col_scaled, signal_value)

    pieces = lax.map(one_block, stacked)
    return pieces.reshape(row_total, col_scaled.shape[1])


def apply_stored(stored, piece):
    return lax.dot_general(
        piece,
        stored,
        (((1,), (1,)), ((), ())),
        precision=lax.Precision.HIGHEST,
        preferred_element_type=jnp.float32,
    )


def body(points, lengthscale, signal, noise, targets, probe_bits):
    scaled = points / lengthscale[:, None]
    signs = 2.0 * probe_bits.astype(jnp.float32) - 1.0
    right_side = jnp.concatenate([targets[None, :], signs], axis=0)
    signal_value = signal[0]
    noise_value = noise[0]
    row_points = collect(scaled, COL, 1)
    col_points = lax.all_gather(scaled, ROW, axis=1, tiled=True)
    stored = build_tile(row_points, col_points, signal_value)
    solution = jnp.zeros_like(right_side)
    residual = right_side
    direction = right_side
    for step in range(ITERS):
        partial_rows = apply_stored(stored, collect(direction, ROW, 1))
        summed = summed_on_arrival(partial_rows, COL, 1)
        image = summed + noise_value * direction
        norm_now, curved, mixed_term, image_sq = (
            by_axis(jnp.sum(residual * residual, axis=1), ROW_COL),
            by_axis(jnp.sum(direction * image, axis=1), ROW_COL),
            by_axis(jnp.sum(residual * image, axis=1), ROW_COL),
            by_axis(jnp.sum(image * image, axis=1), ROW_COL),
        )
        alpha = norm_now / curved
        solution = solution + alpha[:, None] * direction
        residual = residual - alpha[:, None] * image
        if step + 1 < ITERS:
            norm_next = norm_now - 2.0 * alpha * mixed_term + alpha * alpha * image_sq
            direction = residual + (norm_next / norm_now)[:, None] * direction
    return (solution, residual)


def solution(mesh):
    finer = Mesh(mesh.devices.reshape(4, 2, 4, 4), ("row_0", "row_1", "col_0", "col_1"))
    placed = (P(None, ROW_COL), P(), P(), P(), P(ROW_COL), P(None, ROW_COL))
    return jax.shard_map(
        body,
        mesh=finer,
        in_specs=placed,
        out_specs=(P(None, ROW_COL), P(None, ROW_COL)),
        check_vma=False,
    )
```

profile of v0, /device:TPU:0, one launch (start us, length us, event | category | flops | bytes accessed | tf_op | source)
XLA Modules:
  0.0 352.7 jit_solution(1656263548470896958)
XLA Ops:
  0.6 0.8 multiply_add_fusion.6
  1.4 0.7 pad_maximum_fusion
  2.1 0.7 broadcast_in_dim.21
  2.8 4.4 %all-to-all-start = ((f32[8,32,256]{2,1,0:T(8,128)}), f32[8,32,256]{2,1,0:T(8,128)S(1)}, u32[]{:S(2)}, u32[]{:S(2)}) async-start(f32[8,32,256]{2,1,0:T(8,128)} %broadcast_in_dim.21), calls=%async_computation | async-start | bytes 524288 | tf_op jit(solution)/shard_map/all_to_all | solution.py:18
  7.2 0.8 broadcast_divide_fusion
  8.0 6.7 %all-to-all-done = f32[8,32,256]{2,1,0:T(8,128)S(1)} async-done(((f32[8,32,256]{2,1,0:T(8,128)}), f32[8,32,256]{2,1,0:T(8,128)S(1)}, u32[]{:S(2)}, u32[]{:S(2)}) %all-to-all-start) | async-done | bytes 262176 | tf_op jit(solution)/shard_map/all_to_all | solution.py:18
  14.7 0.7 broadcast_in_dim.23
  15.4 8.0 %all-to-all-start.1 = ((f32[16,16,256]{2,1,0:T(8,128)}), f32[16,16,256]{2,1,0:T(8,128)S(1)}, u32[]{:S(2)}, u32[]{:S(2)}) async-start(f32[16,16,256]{2,1,0:T(8,128)} %broadcast_in_dim.23), calls=%async_computation.1 | async-start | bytes 524288 | tf_op jit(solution)/shard_map/all_to_all | solution.py:18
  23.5 12.8 %all_gather.3 = f32[16,2048]{1,0:T(8,128)S(1)} all-gather(f32[16,256]{1,0:T(8,128)S(1)} %broadcast_divide_fusion), channel_id=1, replica_groups=mesh['row_0'=4,'row_1'=2,'col_0'=4,'col_1'=4] {'row_0','row_1'}, dimensions={1}, use_global_device_ids=true | all-gather | bytes 147456 | tf_op jit(solution)/shard_map/all_gather | solution.py:104
  36.3 0.2 copy.9
  36.5 0.0 all-to-all-done.1
  36.5 0.2 copy.10
  36.7 0.1 reshape_reshape.3
  36.8 59.4 %while.12 = (s32[]{:T(128)}, f32[4,1024,2048]{2,1,0:T(8,128)}, f32[]{:T(128)}, f32[4,16,1024]{2,0,1:T(4,128)S(1)}, f32[2048]{0:T(1024)S(1)}, /*index=5*/f32[16,2048]{1,0:T(8,128)S(1)}, s32[]{:T(128)}) while((s32[]{:T(128)}, f32[4,1024,2048]{2,1,0:T(8,128)}, f32[]{:T(128)}, f32[4,16,1024]{2,0,1:T(4,128)S(1)}, f32[2048]{0:T(1024)S(1)}, ...), condition=%wide.region_8.9_spmd, body=%wide.region_6.8_spmd.sunk | while | flops 425753600 | bytes 8799313 | solution.py:83
  36.8 0.1 constant_dynamic-slice_fusion.2
  36.9 14.7 %bitcast_dynamic-update-slice_fusion.2 = f32[4,1024,2048]{2,1,0:T(8,128)} fusion(f32[4,1024,2048]{2,1,0:T(8,128)} %get-tuple-element.192, s32[]{:T(128)} %get-tuple-element.191, f32[16,2048]{1,0:T(8,128)S(1)} %get-tuple-element.203, f32[2048]{0:T(1024)S(1)} %get-tuple-element.202, f32[1024]{0:T(1024)S(1)} %multiply_reduce_fusion.12, ...), kind=kOutput, calls=%fused_computation.clone.1 | convolution fusion | flops 425721856 | bytes 8598528 | tf_op jit(solution)/shard_map/while/body/eval_jaxpr/dot_general | solution.py:53
  51.7 0.1 constant_dynamic-slice_fusion.2
  51.8 14.7 %bitcast_dynamic-update-slice_fusion.2 = f32[4,1024,2048]{2,1,0:T(8,128)} fusion(f32[4,1024,2048]{2,1,0:T(8,128)} %get-tuple-element.192, s32[]{:T(128)} %get-tuple-element.191, f32[16,2048]{1,0:T(8,128)S(1)} %get-tuple-element.203, f32[2048]{0:T(1024)S(1)} %get-tuple-element.202, f32[1024]{0:T(1024)S(1)} %multiply_reduce_fusion.12, ...), kind=kOutput, calls=%fused_computation.clone.1 | convolution fusion | flops 425721856 | bytes 8598528 | tf_op jit(solution)/shard_map/while/body/eval_jaxpr/dot_general | solution.py:53
  66.5 0.1 constant_dynamic-slice_fusion.2
  66.6 14.7 %bitcast_dynamic-update-slice_fusion.2 = f32[4,1024,2048]{2,1,0:T(8,128)} fusion(f32[4,1024,2048]{2,1,0:T(8,128)} %get-tuple-element.192, s32[]{:T(128)} %get-tuple-element.191, f32[16,2048]{1,0:T(8,128)S(1)} %get-tuple-element.203, f32[2048]{0:T(1024)S(1)} %get-tuple-element.202, f32[1024]{0:T(1024)S(1)} %multiply_reduce_fusion.12, ...), kind=kOutput, calls=%fused_computation.clone.1 | convolution fusion | flops 425721856 | bytes 8598528 | tf_op jit(solution)/shard_map/while/body/eval_jaxpr/dot_general | solution.py:53
  81.4 0.1 constant_dynamic-slice_fusion.2
  81.5 14.7 %bitcast_dynamic-update-slice_fusion.2 = f32[4,1024,2048]{2,1,0:T(8,128)} fusion(f32[4,1024,2048]{2,1,0:T(8,128)} %get-tuple-element.192, s32[]{:T(128)} %get-tuple-element.191, f32[16,2048]{1,0:T(8,128)S(1)} %get-tuple-element.203, f32[2048]{0:T(1024)S(1)} %get-tuple-element.202, f32[1024]{0:T(1024)S(1)} %multiply_reduce_fusion.12, ...), kind=kOutput, calls=%fused_computation.clone.1 | convolution fusion | flops 425721856 | bytes 8598528 | tf_op jit(solution)/shard_map/while/body/eval_jaxpr/dot_general | solution.py:53
  96.2 0.0 copy-start
  96.2 34.3 %convolution_bitcast_fusion.2 = f32[16,32,256]{2,1,0:T(8,128)} fusion(f32[32,2048,1]{1,0,2:T(8,128)S(1)} %reshape.171, f32[16,256,2048]{2,1,0:T(8,128)} %bitcast.42), kind=kOutput, calls=%fused_computation.6 | convolution fusion | flops 3221225472 | bytes 34340864 | tf_op jit(solution)/shard_map/dot_general | solution.py:88
  130.5 7.2 %all-to-all-start.2 = ((f32[16,32,256]{2,1,0:T(8,128)}), f32[16,32,256]{2,1,0:T(8,128)S(1)}, u32[]{:S(2)}, u32[]{:S(2)}) async-start(f32[16,32,256]{2,1,0:T(8,128)} %convolution_bitcast_fusion.2), calls=%async_computation.2 | async-start | bytes 1048576 | tf_op jit(solution)/shard_map/all_to_all | solution.py:40
  138.4 11.3 %all-to-all-done.2 = f32[16,32,256]{2,1,0:T(8,128)S(1)} async-done(((f32[16,32,256]{2,1,0:T(8,128)}), f32[16,32,256]{2,1,0:T(8,128)S(1)}, u32[]{:S(2)}, u32[]{:S(2)}) %all-to-all-start.2) | async-done | bytes 524320 | tf_op jit(solution)/shard_map/all_to_all | solution.py:40
  149.8 0.0 copy-done
  149.8 0.2 multiply_reduce_fusion.7
  150.0 8.9 %all-reduce.8 = (f32[32]{0:T(128)S(1)}, f32[32]{0:T(128)S(1)}, f32[32]{0:T(128)S(1)}) all-reduce(f32[32]{0:T(128)S(1)} %get-tuple-element.87, f32[32]{0:T(128)S(1)} %get-tuple-element.82, f32[32]{0:T(128)S(1)} %get-tuple-element.81), channel_id=1, replica_groups=mesh['row_0'=4,'row_1'=2,'col_0'=4,'col_1'=4] {'row_0'}, use_global_device_ids=true, to_apply=%region_1.0 | all-reduce | flops 96 | bytes 768 | tf_op jit(solution)/shard_map/psum | solution.py:46
  158.8 2.5 all-reduce.11
  161.3 8.8 %all-reduce.5 = (f32[32]{0:T(128)S(1)}, f32[32]{0:T(128)S(1)}, f32[32]{0:T(128)S(1)}) all-reduce(f32[32]{0:T(128)S(1)} %get-tuple-element.133, f32[32]{0:T(128)S(1)} %get-tuple-element.134, f32[32]{0:T(128)S(1)} %get-tuple-element.135), channel_id=1, replica_groups=mesh['row_0'=4,'row_1'=2,'col_0'=4,'col_1'=4] {'col_0'}, use_global_device_ids=true, to_apply=%region_3.4 | all-reduce | flops 96 | bytes 768 | tf_op jit(solution)/shard_map/psum | solution.py:46
  170.1 8.4 %all-reduce.2 = (f32[32]{0:T(128)S(1)}, f32[32]{0:T(128)S(1)}, f32[32]{0:T(128)S(1)}) all-reduce(f32[32]{0:T(128)S(1)} %get-tuple-element.115, f32[32]{0:T(128)S(1)} %get-tuple-element.116, f32[32]{0:T(128)S(1)} %get-tuple-element.117), channel_id=1, replica_groups=mesh['row_0'=4,'row_1'=2,'col_0'=4,'col_1'=4] {'col_1'}, use_global_device_ids=true, to_apply=%region_4.5 | all-reduce | flops 96 | bytes 768 | tf_op jit(solution)/shard_map/psum | solution.py:46
  178.5 0.1 multiply_add_fusion.4
  178.6 9.9 %all_to_all.35 = f32[8,32,256]{2,1,0:T(8,128)S(1)} all-to-all(f32[8,32,256]{2,1,0:T(8,128)S(1)} %broadcast_in_dim.24), channel_id=1, replica_groups=mesh['row_0'=4,'row_1'=2,'col_0'=4,'col_1'=4] {'row_0','row_1'}, dimensions={0} | all-to-all | bytes 524288 | tf_op jit(solution)/shard_map/all_to_all | solution.py:18
  188.5 0.2 copy.12
  188.7 33.7 %convolution_bitcast_fusion.1 = f32[16,32,256]{2,1,0:T(8,128)S(1)} fusion(f32[32,2048,1]{1,0,2:T(8,128)S(1)} %reshape.172, f32[16,256,2048]{2,1,0:T(8,128)} %bitcast.43), kind=kOutput, calls=%fused_computation.5 | convolution fusion | flops 3221225472 | bytes 34340864 | tf_op jit(solution)/shard_map/dot_general | solution.py:88
  222.4 14.0 %all_to_all.36 = f32[16,32,256]{2,1,0:T(8,128)S(1)} all-to-all(f32[16,32,256]{2,1,0:T(8,128)S(1)} %convolution_bitcast_fusion.1), channel_id=1, replica_groups=mesh['row_0'=4,'row_1'=2,'col_0'=4,'col_1'=4] {'col_0','col_1'}, dimensions={0} | all-to-all | bytes 1048576 | tf_op jit(solution)/shard_map/all_to_all | solution.py:40
  236.5 0.1 multiply_reduce_fusion.4
  236.7 8.9 %all-reduce.7 = (f32[32]{0:T(128)S(1)}, f32[32]{0:T(128)S(1)}, f32[32]{0:T(128)S(1)}, f32[32]{0:T(128)S(1)}) all-reduce(f32[32]{0:T(128)S(1)} %get-tuple-element.86, f32[32]{0:T(128)S(1)} %get-tuple-element.85, f32[32]{0:T(128)S(1)} %get-tuple-element.84, ...), channel_id=1, replica_groups=mesh['row_0'=4,'row_1'=2,'col_0'=4,'col_1'=4] {'row_0'}, use_global_device_ids=true, to_apply=%region_16.17 | all-reduce | flops 128 | bytes 1024 | tf_op jit(solution)/shard_map/psum | solution.py:46
  245.6 2.5 all-reduce.10
  248.0 8.8 %all-reduce.4 = (f32[32]{0:T(128)S(1)}, f32[32]{0:T(128)S(1)}, f32[32]{0:T(128)S(1)}, f32[32]{0:T(128)S(1)}) all-reduce(f32[32]{0:T(128)S(1)} %get-tuple-element.129, f32[32]{0:T(128)S(1)} %get-tuple-element.130, f32[32]{0:T(128)S(1)} %get-tuple-element.131, ...), channel_id=1, replica_groups=mesh['row_0'=4,'row_1'=2,'col_0'=4,'col_1'=4] {'col_0'}, use_global_device_ids=true, to_apply=%region_18.19 | all-reduce | flops 128 | bytes 1024 | tf_op jit(solution)/shard_map/psum | solution.py:46
  256.8 8.4 %all-reduce.1 = (f32[32]{0:T(128)S(1)}, f32[32]{0:T(128)S(1)}, f32[32]{0:T(128)S(1)}, f32[32]{0:T(128)S(1)}) all-reduce(f32[32]{0:T(128)S(1)} %get-tuple-element.111, f32[32]{0:T(128)S(1)} %get-tuple-element.112, f32[32]{0:T(128)S(1)} %get-tuple-element.113, ...), channel_id=1, replica_groups=mesh['row_0'=4,'row_1'=2,'col_0'=4,'col_1'=4] {'col_1'}, use_global_device_ids=true, to_apply=%region_19.20 | all-reduce | flops 128 | bytes 1024 | tf_op jit(solution)/shard_map/psum | solution.py:46
  265.2 0.2 multiply_reduce_fusion.5
  265.4 0.1 multiply_add_fusion.2
  265.5 9.9 %all_to_all.37 = f32[8,32,256]{2,1,0:T(8,128)S(1)} all-to-all(f32[8,32,256]{2,1,0:T(8,128)S(1)} %broadcast_in_dim.25), channel_id=1, replica_groups=mesh['row_0'=4,'row_1'=2,'col_0'=4,'col_1'=4] {'row_0','row_1'}, dimensions={0} | all-to-all | bytes 524288 | tf_op jit(solution)/shard_map/all_to_all | solution.py:18
  275.4 0.2 copy.13
  275.6 33.7 %convolution_bitcast_fusion = f32[16,32,256]{2,1,0:T(8,128)S(1)} fusion(f32[32,2048,1]{1,0,2:T(8,128)S(1)} %reshape.173, f32[16,256,2048]{2,1,0:T(8,128)} %bitcast.44), kind=kOutput, calls=%fused_computation.4 | convolution fusion | flops 3221225472 | bytes 34340864 | tf_op jit(solution)/shard_map/dot_general | solution.py:88
  309.3 14.0 %all_to_all.38 = f32[16,32,256]{2,1,0:T(8,128)S(1)} all-to-all(f32[16,32,256]{2,1,0:T(8,128)S(1)} %convolution_bitcast_fusion), channel_id=1, replica_groups=mesh['row_0'=4,'row_1'=2,'col_0'=4,'col_1'=4] {'col_0','col_1'}, dimensions={0} | all-to-all | bytes 1048576 | tf_op jit(solution)/shard_map/all_to_all | solution.py:40
  323.4 0.1 multiply_reduce_fusion.2
  323.5 8.9 %all-reduce.6 = (f32[32]{0:T(128)S(1)}, f32[32]{0:T(128)S(1)}) all-reduce(f32[32]{0:T(128)S(1)} %get-tuple-element.136, f32[32]{0:T(128)S(1)} %multiply_reduce_fusion.2), channel_id=1, replica_groups=mesh['row_0'=4,'row_1'=2,'col_0'=4,'col_1'=4] {'row_0'}, use_global_device_ids=true, to_apply=%region_32.33 | all-reduce | flops 64 | bytes 512 | tf_op jit(solution)/shard_map/psum | solution.py:46
  332.4 2.5 all-reduce.9
  334.9 8.8 %all-reduce.3 = (f32[32]{0:T(128)S(1)}, f32[32]{0:T(128)S(1)}) all-reduce(f32[32]{0:T(128)S(1)} %get-tuple-element.127, f32[32]{0:T(128)S(1)} %get-tuple-element.128), channel_id=1, replica_groups=mesh['row_0'=4,'row_1'=2,'col_0'=4,'col_1'=4] {'col_0'}, use_global_device_ids=true, to_apply=%region_34.35 | all-reduce | flops 64 | bytes 512 | tf_op jit(solution)/shard_map/psum | solution.py:46
  343.7 8.3 %all-reduce = (f32[32]{0:T(128)S(1)}, f32[32]{0:T(128)S(1)}) all-reduce(f32[32]{0:T(128)S(1)} %get-tuple-element.109, f32[32]{0:T(128)S(1)} %get-tuple-element.110), channel_id=1, replica_groups=mesh['row_0'=4,'row_1'=2,'col_0'=4,'col_1'=4] {'col_1'}, use_global_device_ids=true, to_apply=%region_35.36 | all-reduce | flops 64 | bytes 512 | tf_op jit(solution)/shard_map/psum | solution.py:46
  352.0 0.7 multiply_subtract_fusion
  (17 shorter events, 0.4 us)
Async XLA Ops:
  2.8 11.9 %all-to-all-start = ((f32[8,32,256]{2,1,0:T(8,128)}), f32[8,32,256]{2,1,0:T(8,128)S(1)}, u32[]{:S(2)}, u32[]{:S(2)}) async-start(f32[8,32,256]{2,1,0:T(8,128)} %broadcast_in_dim.21), calls=%async_computation | async-start | bytes 524288 | tf_op jit(solution)/shard_map/all_to_all | solution.py:18
  15.4 21.1 %all-to-all-start.1 = ((f32[16,16,256]{2,1,0:T(8,128)}), f32[16,16,256]{2,1,0:T(8,128)S(1)}, u32[]{:S(2)}, u32[]{:S(2)}) async-start(f32[16,16,256]{2,1,0:T(8,128)} %broadcast_in_dim.23), calls=%async_computation.1 | async-start | bytes 524288 | tf_op jit(solution)/shard_map/all_to_all | solution.py:18
  96.2 53.6 %copy-start = (f32[256]{0:T(256)S(1)}, f32[256]{0:T(256)}, u32[]{:S(2)}) copy-start(f32[256]{0:T(256)} %param.12) | copy-start | bytes 3076
  130.5 19.2 %all-to-all-start.2 = ((f32[16,32,256]{2,1,0:T(8,128)}), f32[16,32,256]{2,1,0:T(8,128)S(1)}, u32[]{:S(2)}, u32[]{:S(2)}) async-start(f32[16,32,256]{2,1,0:T(8,128)} %convolution_bitcast_fusion.2), calls=%async_computation.2 | async-start | bytes 1048576 | tf_op jit(solution)/shard_map/all_to_all | solution.py:40
where the time goes:
time: 354 us; the launch traced here: 353 us
  matrix products  161 us (45%)
  blocking collectives  146 us (41%)
  starting transfers between devices  19.7 us (6%)
  waiting for transfers between devices  18.1 us (5%)
  other arithmetic  3.96 us (1%)
    dot_general x3, matrix products, apply_stored(): lax.dot_general(piece, stored, (((1,), (1,)), ((), ())), precision=lax.Pr...  102 us
    psum x12, blocking collectives, by_axis(): x = lax.psum(x, axis)  85.5 us
    dot_general x4, matrix products, matern_tile(): lax.dot_general(row_scaled, col_scaled, (((0,), (0,)), ((), ())), precisi...  58.9 us
    all_to_all x2, blocking collectives, summed_on_arrival(): tiles = lax.all_to_all(in_blocks(x, dim, length), axis, 0, 0, tiled=True)  28.1 us
    all_to_all x2, blocking collectives, copy_for_each(): lax.all_to_all(jnp.broadcast_to(x[None], (length, *x.shape)), axis, 0, 0,...  19.8 us
    all_gather x1, blocking collectives, body(): col_points = lax.all_gather(scaled, ROW, axis=1, tiled=True)  12.8 us
    all_to_all x2, starting transfers between devices, copy_for_each(): lax.all_to_all(jnp.broadcast_to(x[None], (length, *x.shape)), axis, 0, 0,...  12.5 us
    all_to_all x1, waiting for transfers between devices, summed_on_arrival(): tiles = lax.all_to_all(in_blocks(x, dim, length), axis, 0, 0, tiled=True)  11.3 us
  transfers between devices with their start and end apart: 3, of which 2 were waited for; matrix products, arithmetic and copies ran while one was open for 0% of the time, Pallas kernels for 0%

commit v1 on v0

v1 whole, which is shorter than its diff:
```python
import functools
import math

import jax
import jax.numpy as jnp
from jax import lax
from jax.experimental import pallas as pl
from jax.experimental.pallas import tpu as pltpu
from jax.sharding import PartitionSpec as P

ITERS = 3
F32 = jnp.float32
BF16 = jnp.bfloat16
MESH = pl.DeviceIdType.MESH
LN2 = math.log(2.0)
SPREAD = math.sqrt(5.0) / LN2
LINEAR = 3.0 / LN2
CONSTANT = 3.0 / LN2**2
CHUNK = 512


def pieces(x):
    first = x.astype(BF16).astype(F32)
    rest = x - first
    second = rest.astype(BF16).astype(F32)
    return first, second, (rest - second).astype(BF16).astype(F32)


def with_norms(x, before, after):
    parts = pieces(jnp.sum(x * x, axis=0, keepdims=True))
    row = lax.broadcasted_iota(jnp.int32, x.shape, 0)
    out = jnp.where((row >= after) & (row < after + 3), 1.0, 0.0)
    for i, part in enumerate(parts):
        out = jnp.where(row == before + i, part, out)
    return out


def left_operand(x):
    one, two, three = (-2.0 * p for p in pieces(x))
    return jnp.concatenate([one, one, two, two, one, three, with_norms(x, 0, 3), jnp.zeros_like(x)], axis=0)


def right_operand(x):
    one, two, three = pieces(x)
    return jnp.concatenate([one, two, one, two, three, one, with_norms(x, 3, 0), jnp.zeros_like(x)], axis=0)


def dot(a, b):
    return lax.dot_general(a, b, (((1,), (0,)), ((), ())), preferred_element_type=F32)


def kernel(rows, cols, points, scales, signal, noise, targets, bits, out_x, out_r,
           mine, near, far, left, right, upper, lower, even, odd, vectors, resid, direc, steps, part, landed, images, tell, told,
           near_sem, far_sem, land_sem, image_sem, told_sem, sent):
    n = points.shape[1]
    pairs = rows // 2
    width = 2 * n
    depth = cols * n
    chunks = depth // CHUNK
    row, col = lax.axis_index("row"), lax.axis_index("col")
    here = row * cols + col
    count = rows * cols

    def remote(src, dst, send, recv, r, c):
        return pltpu.make_async_remote_copy(
            src_ref=src, dst_ref=dst, send_sem=send, recv_sem=recv, device_id={"row": r, "col": c}, device_id_type=MESH)

    def await_bytes(ref, sem):
        pltpu.make_async_copy(ref, ref, sem).wait()

    def each(lo, hi, fn):
        def step(i, carry):
            fn(i)
            return carry
        lax.fori_loop(lo, hi, step, 0)

    barrier = pltpu.get_barrier_semaphore()

    def greet(i):
        t = lax.rem(here + i, count)
        pl.semaphore_signal(barrier, inc=1, device_id={"row": t // cols, "col": lax.rem(t, cols)}, device_id_type=MESH)

    each(1, count, greet)
    mine[0:16, :] = points[...] / scales[...] * SPREAD
    mine[16:17, :] = targets[...]
    mine[17:48, :] = 2.0 * bits[...].astype(F32) - 1.0
    near[col] = mine[...]
    far[row] = mine[0:16, :]
    steps[...] = jnp.zeros_like(steps)
    pl.semaphore_wait(barrier, count - 1)

    def send_near(i):
        c = lax.rem(col + i, cols)
        remote(mine, near.at[col], sent.at[0], near_sem.at[col], row, c).start()

    def send_far(i):
        r = lax.rem(row + i, rows)
        remote(mine.at[0:16], far.at[row], sent.at[1], far_sem.at[row], r, col).start()

    each(1, rows, send_far)
    each(1, cols, send_near)

    def split_into(j, d):
        at = pl.ds(pl.multiple_of(j * n, n), n)
        one, two, three = pieces(d)
        vectors[0:32, at] = one.astype(BF16)
        vectors[32:64, at] = two.astype(BF16)
        vectors[64:96, at] = three.astype(BF16)

    def take_near(i):
        j = lax.rem(col + i, cols)

        @pl.when(i > 0)
        def _():
            remote(mine, near.at[j], sent.at[0], near_sem.at[j], row, j).wait_recv()

        block = near[j]
        left[pl.ds(pl.multiple_of(j * n, n), n), :] = jnp.transpose(left_operand(block[0:16])).astype(BF16)
        resid[j] = block[16:48]
        direc[j] = block[16:48]
        split_into(j, block[16:48])

    def take_far(i):
        j = lax.rem(row + i, rows)

        @pl.when(i > 0)
        def _():
            remote(mine.at[0:16], far.at[j], sent.at[1], far_sem.at[j], j, col).wait_recv()

        right[j // 2, :, pl.ds(pl.multiple_of(lax.rem(j, 2) * n, n), n)] = right_operand(far[j]).astype(BF16)

    each(0, rows, take_far)
    each(0, cols, take_near)

    amplitude = jnp.log(jnp.full((1, width), signal[0], F32)) * (1.0 / LN2) - math.log2(CONSTANT)

    def distances(p, c):
        return dot(left[pl.ds(pl.multiple_of(c * CHUNK, CHUNK), CHUNK), :], right[p])

    def evaluate(buffer, p, c):
        for at in range(0, CHUNK, 32):
            u = jnp.maximum(buffer[at : at + 32, :], 1e-30)
            q = u * lax.rsqrt(u)
            value = ((q + LINEAR) * q + CONSTANT) * jnp.exp2(amplitude - q)
            high = value.astype(BF16)
            to = pl.ds(pl.multiple_of(c * CHUNK + at, 32), 32)
            upper[p, to, :] = high
            lower[p, to, :] = (value - high.astype(F32)).astype(BF16)

    def build(p):
        even[...] = distances(p, 0)

        def step(i):
            odd[...] = distances(p, 2 * i + 1)
            evaluate(even, p, 2 * i)
            even[...] = distances(p, lax.rem(2 * i + 2, chunks))
            evaluate(odd, p, 2 * i + 1)

        each(0, chunks // 2, step)

    each(0, pairs, build)

    def image_at_home(k):
        def step(s):
            p = lax.rem(row // 2 + 1 + s, pairs)
            big = dot(vectors[...], upper[p])
            small = dot(vectors[0:64, :], lower[p])
            total = big[0:32] + (big[32:64] + small[0:32] + (big[64:96] + small[32:64]))
            for core in range(2):
                r = 2 * p + core
                part[k, r] = total[:, core * n : core * n + n]

                @pl.when(r != row)
                def _():
                    slot = lax.rem(row - r + 2 * rows - 1, rows)
                    remote(part.at[k, r], landed.at[k, slot], sent.at[2 + k], land_sem.at[k], r, col).start()

        each(0, pairs, step)
        await_bytes(landed.at[k], land_sem.at[k])
        total = part[k, row]
        for slot in range(rows - 1):
            total = total + landed[k, slot]
        return total + noise[0] * direc[col]

    for k in range(ITERS):
        image = image_at_home(k)
        d, r = direc[col], resid[col]
        sums = [jnp.sum(a, axis=1, keepdims=True) for a in (d * image, r * image, image * image, r * r)]
        turned = jnp.transpose(jnp.broadcast_to(jnp.concatenate(sums, axis=0), (128, 128)))
        tell[k, 0:1] = turned[0:1]
        told[k, pl.ds(here, 1)] = turned[0:1]

        def send_tell(i):
            t = lax.rem(here + i, count)
            remote(tell.at[k, 0:1], told.at[k, pl.ds(here, 1)], sent.at[5 + k], told_sem.at[k],
                   t // cols, lax.rem(t, cols)).start()

        each(1, count, send_tell)
        if k + 1 < ITERS:
            images[k, col] = image

            def send_image(i):
                c = lax.rem(col + i, cols)
                remote(images.at[k, col], images.at[k, col], sent.at[8 + k], image_sem.at[k, col], row, c).start()

            each(1, cols, send_image)
        await_bytes(told.at[k, 0 : count - 1], told_sem.at[k])
        total = jnp.sum(told[k], axis=0, keepdims=True)
        turned = jnp.transpose(jnp.broadcast_to(total, (128, 128)))
        curved, mixed, square, norm = (turned[32 * i : 32 * i + 32] for i in range(4))
        alpha = norm / curved
        following = norm - 2.0 * alpha * mixed + alpha * alpha * square
        beta = following / norm
        alpha = jnp.concatenate([alpha] * (n // 128), axis=1)
        beta = jnp.concatenate([beta] * (n // 128), axis=1)
        steps[...] = steps[...] + alpha * d
        if k + 1 == ITERS:
            out_x[...] = steps[...]
            out_r[...] = r - alpha * image
        else:
            def take_image(i):
                j = lax.rem(col + i, cols)

                @pl.when(i > 0)
                def _():
                    remote(images.at[k, j], images.at[k, j], sent.at[8 + k], image_sem.at[k, j], row, j).wait_recv()

                rest = resid[j] - alpha * images[k, j]
                onward = rest + beta * direc[j]
                resid[j] = rest
                direc[j] = onward
                split_into(j, onward)

            each(0, cols, take_image)

    await_bytes(near.at[0 : cols - 1], sent.at[0])
    await_bytes(far.at[0 : rows - 1], sent.at[1])
    for k in range(ITERS):
        await_bytes(landed.at[k], sent.at[2 + k])
        await_bytes(told.at[k, 0 : count - 1], sent.at[5 + k])
        if k + 1 < ITERS:
            await_bytes(images.at[k, 0 : cols - 1], sent.at[8 + k])


def solution(mesh):
    rows, cols = mesh.shape["row"], mesh.shape["col"]
    pairs = rows // 2

    def body(points, lengthscale, signal, noise, targets, probe_bits):
        n = points.shape[1]
        depth, width, block = cols * n, 2 * n, (32, n)
        vmem = pl.BlockSpec(memory_space=pltpu.VMEM)
        smem = pl.BlockSpec(memory_space=pltpu.SMEM)
        return pl.pallas_call(
            functools.partial(kernel, rows, cols),
            out_shape=(jax.ShapeDtypeStruct(block, F32),) * 2,
            in_specs=[vmem, vmem, smem, smem, vmem, vmem],
            out_specs=(vmem, vmem),
            scratch_shapes=[
                pltpu.VMEM((48, n), F32),
                pltpu.VMEM((cols, 48, n), F32),
                pltpu.VMEM((rows, 16, n), F32),
                pltpu.VMEM((depth, 128), BF16),
                pltpu.VMEM((pairs, 128, width), BF16),
                pltpu.VMEM((pairs, depth, width), BF16),
                pltpu.VMEM((pairs, depth, width), BF16),
                pltpu.VMEM((CHUNK, width), F32),
                pltpu.VMEM((CHUNK, width), F32),
                pltpu.VMEM((96, depth), BF16),
                pltpu.VMEM((cols, *block), F32),
                pltpu.VMEM((cols, *block), F32),
                pltpu.VMEM(block, F32),
                pltpu.VMEM((ITERS, rows, *block), F32),
                pltpu.VMEM((ITERS, rows - 1, *block), F32),
                pltpu.VMEM((ITERS - 1, cols, *block), F32),
                pltpu.VMEM((ITERS, 8, 128), F32),
                pltpu.VMEM((ITERS, rows * cols, 128), F32),
                pltpu.SemaphoreType.DMA((cols,)),
                pltpu.SemaphoreType.DMA((rows,)),
                pltpu.SemaphoreType.DMA((ITERS,)),
                pltpu.SemaphoreType.DMA((ITERS - 1, cols)),
                pltpu.SemaphoreType.DMA((ITERS,)),
                pltpu.SemaphoreType.DMA((10,)),
            ],
            compiler_params=pltpu.CompilerParams(
                collective_id=0, has_side_effects=True, vmem_limit_bytes=60 * 1024 * 1024),
        )(points, lengthscale[:, None], signal, noise, targets[None, :], probe_bits)

    both = ("row", "col")
    placed = (P(None, both), P(), P(), P(), P(both), P(None, both))
    return jax.shard_map(body, mesh=mesh, in_specs=placed, out_specs=(P(None, both),) * 2, check_vma=False)
```

time: 354 us -> 111 us (0.31)
  matrix products: 161 us -> 0 us
  blocking collectives: 146 us -> 0 us
  Pallas kernels: 0 us -> 105 us
  starting transfers between devices: 19.7 us -> 0 us
  waiting for transfers between devices: 18.1 us -> 0 us
  other arithmetic: 3.96 us -> 0 us
    dot_general x7 -> x0, matrix products: 161 us -> none  [the longest x3 102 us: apply_stored(): lax.dot_general(piece, stored, (((1,), (1,)), ((), ())), precision=lax.Pr...]
    pallas_call x0 -> x1, Pallas kernels: none -> 105 us  [body(): pl.pallas_call(functools.partial(kernel, rows, cols), out_shape=(jax.Shap...]
    psum x12 -> x0, blocking collectives: 85.5 us -> none  [by_axis(): x = lax.psum(x, axis)]
    all_to_all x4 -> x0, blocking collectives: 47.9 us -> none  [the longest x2 28.1 us: summed_on_arrival(): tiles = lax.all_to_all(in_blocks(x, dim, length), axis, 0, 0, tiled=True)]
    all_to_all x3 -> x0, starting transfers between devices: 19.7 us -> none  [the longest x2 12.5 us: copy_for_each(): lax.all_to_all(jnp.broadcast_to(x[None], (length, *x.shape)), axis, 0, 0,...]
    all_to_all x3 -> x0, waiting for transfers between devices: 18.1 us -> none  [the longest x1 11.3 us: summed_on_arrival(): tiles = lax.all_to_all(in_blocks(x, dim, length), axis, 0, 0, tiled=True)]
    all_gather x1 -> x0, blocking collectives: 12.8 us -> none  [body(): col_points = lax.all_gather(scaled, ROW, axis=1, tiled=True)]
  transfers between devices with their start and end apart: 3 -> 0, of which waited for: 2 -> 0; matrix products, arithmetic and copies ran while one was open for 0% -> 0% of each run, Pallas kernels for 0% -> 0%
where the time goes in v1:
time: 111 us; the launch traced here: 110 us
  Pallas kernels  105 us (95%)
  local copies, waits for them, and re-layouts  3.33 us (3%)
  between operations  1.95 us (2%)
    pallas_call x1, Pallas kernels, body(): pl.pallas_call(functools.partial(kernel, rows, cols), out_shape=(jax.Shap...  105 us
    unnamed x6, local copies, waits for them, and re-layouts  2.65 us

profile of v1, /device:TPU:0, one launch (start us, length us, event | category | flops | bytes accessed | tf_op | source)
XLA Modules:
  0.0 110.0 jit_solution(10256623012395516075)
XLA Ops:
  1.9 0.0 copy-start.1
  1.9 0.6 copy-done.1
  2.6 0.7 copy.8.scales
  3.3 104.8 %shard_map.77 = (f32[32,256]{1,0:T(8,128)}, f32[32,256]{1,0:T(8,128)}) custom-call(f32[16,256]{1,0:T(8,128)} %points.1, f32[16,1]{1,0:T(8,128)} %copy.8.scales, f32[1]{0:T(128)S(6)} %copy.11.signal, f32[1]{0:T(128)S(6)} %copy.12.noise, f32[1,256]{1,0:T(1,128)} %bitcast.2, s32[31,256]{1,0:T(8,128)} %bits.1), custom_call_target="tpu_custom_call" | custom-call | tf_op jit(solution)/shard_map/pallas_call | solution.py:254
  108.0 0.0 copy-start
  108.0 1.4 %copy.13 = f32[32,256]{1,0:T(8,128)} copy(f32[32,256]{1,0:T(8,128)} %get-tuple-element.4) | data formatting | bytes 65536
  109.4 0.0 copy-done
  109.4 0.6 copy.14
Async XLA Ops:
  1.9 0.7 copy-start.1
  108.0 1.4 %copy-start = (f32[32,256]{1,0:T(8,128)S(1)}, f32[32,256]{1,0:T(8,128)}, u32[]{:S(2)}) copy-start(f32[32,256]{1,0:T(8,128)} %get-tuple-element.5) | copy-start | bytes 98308

commit v2 on v1

v2 whole, which is shorter than its diff:
```python
import functools
import math

import jax
import jax.numpy as jnp
from jax import lax
from jax.experimental import pallas as pl
from jax.experimental.pallas import tpu as pltpu
from jax.sharding import PartitionSpec as P

F32 = jnp.float32
BF16 = jnp.bfloat16
MESH = pl.DeviceIdType.MESH
LN2 = math.log(2.0)
SPREAD = math.sqrt(5.0) / LN2
LINEAR = 3.0 / LN2
CONSTANT = 3.0 / LN2**2
CHUNK = 512


def pieces(x):
    first = x.astype(BF16).astype(F32)
    rest = x - first
    second = rest.astype(BF16).astype(F32)
    return first, second, (rest - second).astype(BF16).astype(F32)


def with_norms(x, before, after):
    parts = pieces(jnp.sum(x * x, axis=0, keepdims=True))
    row = lax.broadcasted_iota(jnp.int32, x.shape, 0)
    out = jnp.where((row >= after) & (row < after + 3), 1.0, 0.0)
    for i, part in enumerate(parts):
        out = jnp.where(row == before + i, part, out)
    return out


def left_operand(x):
    one, two, three = (-2.0 * p for p in pieces(x))
    return jnp.concatenate([one, one, two, two, one, three, with_norms(x, 0, 3), jnp.zeros_like(x)], axis=0)


def right_operand(x):
    one, two, three = pieces(x)
    return jnp.concatenate([one, two, one, two, three, one, with_norms(x, 3, 0), jnp.zeros_like(x)], axis=0)


def dot(a, b):
    return lax.dot_general(a, b, (((1,), (0,)), ((), ())), preferred_element_type=F32)


def flipped(v):
    return v + 1 - 2 * lax.rem(v, 2)


def turned(v):
    return lax.rem(v + 2 * lax.rem(v, 2) + 3, 4)


def kernel(rings, points, scales, signal, noise, targets, bits, out_x, out_r,
           mine, mine_b, near, near_b, far, left, right, upper, lower, even, odd, vectors, sums, part, landed, gathered,
           met, summed, near_sem, far_sem, land_sem, gather_sem, relay_sem, met_sem, summed_sem, sent):
    n = points.shape[1]
    cube = 2**rings
    pairs = cube // 2
    width = 2 * n
    depth = 2 * cube * n
    chunks = depth // CHUNK
    row, col = lax.axis_index("row"), lax.axis_index("col")
    core = lax.rem(row, 2)
    place = [row // 2]
    for i in range(rings - 1):
        place.append(lax.rem(col // 4 ** (rings - 2 - i), 4))

    def device(places, core):
        c = 0
        for v in places[1:]:
            c = 4 * c + v
        return {"row": 2 * places[0] + core, "col": c}

    def gather_partner(mask, other):
        return device([flipped(v) if mask >> i & 1 else v for i, v in enumerate(place)], 1 - core if other else core)

    def reduce_partner(mask):
        return device([v + lax.rem(mask // 2**i, 2) * (turned(v) - v) for i, v in enumerate(place)], core)

    def remote(src, dst, send, recv, to):
        return pltpu.make_async_remote_copy(
            src_ref=src, dst_ref=dst, send_sem=send, recv_sem=recv, device_id=to, device_id_type=MESH)

    def await_bytes(ref, sem):
        pltpu.make_async_copy(ref, ref, sem).wait()

    def each(lo, hi, fn):
        def step(i, carry):
            fn(i)
            return carry
        lax.fori_loop(lo, hi, step, 0)

    near_masks = sorted(range(1, cube), key=lambda m: (-bin(m).count("1"), m))
    slots = [(m, f) for m in near_masks for f in range(2)] + [(0, 1)]

    barrier = pltpu.get_barrier_semaphore()
    for m, f in slots:
        pl.semaphore_signal(barrier, inc=1, device_id=gather_partner(m, f), device_id_type=MESH)
    for m in near_masks:
        pl.semaphore_signal(barrier, inc=1, device_id=reduce_partner(m), device_id_type=MESH)
    x = points[...] / scales[...] * SPREAD
    mine[...] = x
    near[0] = x
    far[cube - 1] = x
    mine_b[0:1, :] = targets[...]
    mine_b[1:32, :] = 2.0 * bits[...].astype(F32) - 1.0
    near_b[0] = mine_b[...]
    pl.semaphore_wait(barrier, len(slots) + len(near_masks))

    for m, f in slots:
        remote(mine, near.at[f * cube + m], sent.at[0], near_sem.at[0], gather_partner(m, f)).start()
    for m in near_masks:
        remote(mine, far.at[cube - 1 - m], sent.at[1], far_sem.at[0], reduce_partner(m)).start()
    for m, f in slots:
        remote(mine_b, near_b.at[f * cube + m], sent.at[2], near_sem.at[1], gather_partner(m, f)).start()

    def split_into(slot, d):
        at = pl.ds(pl.multiple_of(slot * n, n), n)
        high = d.astype(BF16)
        vectors[0:32, at] = high
        vectors[32:64, at] = (d - high.astype(F32)).astype(BF16)

    def place_left(i):
        left[pl.ds(pl.multiple_of(i * n, n), n), :] = jnp.transpose(left_operand(near[i])).astype(BF16)

    def place_right(i):
        right[i // 2, :, pl.ds(pl.multiple_of(lax.rem(i, 2) * n, n), n)] = right_operand(far[i]).astype(BF16)

    await_bytes(far.at[0 : cube - 1], far_sem.at[0])
    each(0, cube, place_right)
    await_bytes(near.at[1 : 2 * cube], near_sem.at[0])
    each(0, 2 * cube, place_left)

    amplitude = jnp.log(jnp.full((1, width), signal[0], F32)) * (1.0 / LN2) - math.log2(CONSTANT)

    def distances(p, c):
        return dot(left[pl.ds(pl.multiple_of(c * CHUNK, CHUNK), CHUNK), :], right[p])

    def evaluate(buffer, p, c):
        for at in range(0, CHUNK, 32):
            u = jnp.maximum(buffer[at : at + 32, :], 1e-30)
            q = u * lax.rsqrt(u)
            value = ((q + LINEAR) * q + CONSTANT) * jnp.exp2(amplitude - q)
            high = value.astype(BF16)
            to = pl.ds(pl.multiple_of(c * CHUNK + at, 32), 32)
            upper[p, to, :] = high
            lower[p, to, :] = (value - high.astype(F32)).astype(BF16)

    def product(p, at):
        big = dot(vectors[:, at], upper[p, at, :])
        small = dot(vectors[0:32, at], lower[p, at, :])
        return big[0:32] + (big[32:64] + small)

    def send_parts(k, p, total):
        for j in range(2):
            slot = 2 * p + j
            part[k, slot] = total[:, j * n : j * n + n]

            def send():
                remote(part.at[k, slot], landed.at[k, slot], sent.at[3 + k], land_sem.at[k],
                       reduce_partner(cube - 1 - slot)).start()

            if isinstance(p, int):
                if slot < cube - 1:
                    send()
            elif j == 0:
                send()
            else:
                pl.when(p < pairs - 1)(send)

    even[...] = distances(0, 0)
    for p in range(pairs):
        if p == 1:
            await_bytes(near_b.at[1 : 2 * cube], near_sem.at[1])
            each(0, 2 * cube, lambda i: split_into(i, near_b[i]))
        if p:
            sums[...] = jnp.zeros_like(sums)

        def step(i):
            odd[...] = distances(p, 2 * i + 1)
            evaluate(even, p, 2 * i)
            even[...] = distances(jnp.minimum(p + (2 * i + 2) // chunks, pairs - 1), lax.rem(2 * i + 2, chunks))
            evaluate(odd, p, 2 * i + 1)
            if p:
                sums[...] = sums[...] + product(p - 1, pl.ds(pl.multiple_of(2 * i * CHUNK, 2 * CHUNK), 2 * CHUNK))

        each(0, chunks // 2, step)
        if p:
            send_parts(0, p - 1, sums[...])
    if pairs == 1:
        await_bytes(near_b.at[1 : 2 * cube], near_sem.at[1])
        each(0, 2 * cube, lambda i: split_into(i, near_b[i]))
    send_parts(0, pairs - 1, product(pairs - 1, pl.ds(0, depth)))

    def multiply(k):
        each(0, pairs, lambda p: send_parts(k, p, product(p, pl.ds(0, depth))))

    def at_home(k, v):
        await_bytes(landed.at[k], land_sem.at[k])
        total = part[k, cube - 1]
        for slot in range(cube - 1):
            total = total + landed[k, slot]
        return total + noise[0] * v

    def gather(k, w):
        gathered[k, 0] = w
        for m in near_masks:
            remote(gathered.at[k, 0], gathered.at[k, m], sent.at[6 + k], gather_sem.at[k, m], gather_partner(m, 0)).start()
        remote(gathered.at[k, 0], gathered.at[k, cube], sent.at[6 + k], relay_sem.at[k], gather_partner(0, 1)).start()

    def take_gathered(k):
        split_into(0, gathered[k, 0])
        for m in reversed(near_masks):
            remote(gathered.at[k, 0], gathered.at[k, m], sent.at[6 + k], gather_sem.at[k, m], gather_partner(m, 0)).wait_recv()
            remote(gathered.at[k, m], gathered.at[k, cube + m], sent.at[6 + k], relay_sem.at[k], gather_partner(0, 1)).start()
            split_into(m, gathered[k, m])
        await_bytes(gathered.at[k, cube : 2 * cube], relay_sem.at[k])
        each(cube, 2 * cube, lambda i: split_into(i, gathered[k, i]))

    def tell(k, r, w):
        both = [jnp.sum(a, axis=1, keepdims=True) for a in (r * r, w * r)]
        column = jnp.concatenate(both + [jnp.zeros((64, 1), F32)], axis=0)
        met[k, 0:1] = jnp.transpose(jnp.broadcast_to(column, (128, 128)))[0:1]
        for m, f in slots:
            at = f * cube + m
            remote(met.at[k, 0:1], met.at[k, at : at + 1], sent.at[8 + k], met_sem.at[k], gather_partner(m, f)).start()

    def pass_on(k):
        await_bytes(met.at[k, 1 : 2 * cube], met_sem.at[k])
        summed[k, cube - 1 : cube] = jnp.sum(met[k], axis=0, keepdims=True)
        for m in near_masks:
            at = cube - 1 - m
            remote(summed.at[k, cube - 1 : cube], summed.at[k, at : at + 1], sent.at[11 + k], summed_sem.at[k],
                   reduce_partner(m)).start()

    def hear(k):
        await_bytes(summed.at[k, 0 : cube - 1], summed_sem.at[k])
        total = jnp.sum(summed[k], axis=0, keepdims=True)
        spread = jnp.transpose(jnp.broadcast_to(total, (128, 128)))
        return [jnp.concatenate([spread[32 * i : 32 * i + 32]] * (n // 128), axis=1) for i in range(2)]

    r = near_b[0]
    w = at_home(0, r)
    gather(0, w)
    tell(0, r, w)
    take_gathered(0)
    pass_on(0)
    multiply(1)
    z = at_home(1, w)
    norm, curved = hear(0)
    alpha = norm / curved
    p, s = r, w
    r, w_next = r - alpha * s, w - alpha * z
    gather(1, w_next)
    tell(1, r, w_next)
    x = alpha * p
    take_gathered(1)
    pass_on(1)
    multiply(2)
    w = w_next
    q = at_home(2, w)
    following, curved = hear(1)
    beta = following / norm
    norm, alpha = following, following / (curved - beta * following / alpha)
    p, s, z = r + beta * p, w + beta * s, q + beta * z
    r, w = r - alpha * s, w - alpha * z
    tell(2, r, w)
    x = x + alpha * p
    pass_on(2)
    following, curved = hear(2)
    beta = following / norm
    alpha = following / (curved - beta * following / alpha)
    out_x[...] = x + alpha * (r + beta * p)
    out_r[...] = r - alpha * (w + beta * s)

    await_bytes(near.at[1 : 2 * cube], sent.at[0])
    await_bytes(far.at[0 : cube - 1], sent.at[1])
    await_bytes(near_b.at[1 : 2 * cube], sent.at[2])
    for k in range(3):
        await_bytes(landed.at[k], sent.at[3 + k])
        await_bytes(met.at[k, 1 : 2 * cube], sent.at[8 + k])
        await_bytes(summed.at[k, 0 : cube - 1], sent.at[11 + k])
    for k in range(2):
        await_bytes(gathered.at[k, 1 : 2 * cube], sent.at[6 + k])


def solution(mesh):
    rings = {1: 1, 4: 2, 16: 3}[mesh.shape["col"]]
    cube = 2**rings

    def body(points, lengthscale, signal, noise, targets, probe_bits):
        n = points.shape[1]
        depth, width, block = 2 * cube * n, 2 * n, (32, n)
        vmem = pl.BlockSpec(memory_space=pltpu.VMEM)
        smem = pl.BlockSpec(memory_space=pltpu.SMEM)
        return pl.pallas_call(
            functools.partial(kernel, rings),
            out_shape=(jax.ShapeDtypeStruct(block, F32),) * 2,
            in_specs=[vmem, vmem, smem, smem, vmem, vmem],
            out_specs=(vmem, vmem),
            scratch_shapes=[
                pltpu.VMEM((16, n), F32),
                pltpu.VMEM(block, F32),
                pltpu.VMEM((2 * cube, 16, n), F32),
                pltpu.VMEM((2 * cube, *block), F32),
                pltpu.VMEM((cube, 16, n), F32),
                pltpu.VMEM((depth, 128), BF16),
                pltpu.VMEM((cube // 2, 128, width), BF16),
                pltpu.VMEM((cube // 2, depth, width), BF16),
                pltpu.VMEM((cube // 2, depth, width), BF16),
                pltpu.VMEM((CHUNK, width), F32),
                pltpu.VMEM((CHUNK, width), F32),
                pltpu.VMEM((64, depth), BF16),
                pltpu.VMEM((32, width), F32),
                pltpu.VMEM((3, cube, *block), F32),
                pltpu.VMEM((3, cube - 1, *block), F32),
                pltpu.VMEM((2, 2 * cube, *block), F32),
                pltpu.VMEM((3, 2 * cube, 128), F32),
                pltpu.VMEM((3, cube, 128), F32),
                pltpu.SemaphoreType.DMA((2,)),
                pltpu.SemaphoreType.DMA((1,)),
                pltpu.SemaphoreType.DMA((3,)),
                pltpu.SemaphoreType.DMA((2, cube)),
                pltpu.SemaphoreType.DMA((2,)),
                pltpu.SemaphoreType.DMA((3,)),
                pltpu.SemaphoreType.DMA((3,)),
                pltpu.SemaphoreType.DMA((14,)),
            ],
            compiler_params=pltpu.CompilerParams(
                collective_id=0, has_side_effects=True, vmem_limit_bytes=60 * 1024 * 1024),
        )(points, lengthscale[:, None], signal, noise, targets[None, :], probe_bits)

    both = ("row", "col")
    placed = (P(None, both), P(), P(), P(), P(both), P(None, both))
    return jax.shard_map(body, mesh=mesh, in_specs=placed, out_specs=(P(None, both),) * 2, check_vma=False)
```

time: 111 us -> 91.3 us (0.82)
  Pallas kernels: 105 us -> 85.7 us
    pallas_call x1, Pallas kernels: 105 us -> 85.7 us  [body(): pl.pallas_call(functools.partial(kernel, rings), out_shape=(jax.ShapeDtyp...]
where the time goes in v2:
time: 91.3 us; the launch traced here: 91 us
  Pallas kernels  85.7 us (94%)
  local copies, waits for them, and re-layouts  3.33 us (4%)
  between operations  1.95 us (2%)
    pallas_call x1, Pallas kernels, body(): pl.pallas_call(functools.partial(kernel, rings), out_shape=(jax.ShapeDtyp...  85.7 us
    unnamed x6, local copies, waits for them, and re-layouts  2.65 us

profile of v2, /device:TPU:0, one launch (start us, length us, event | category | flops | bytes accessed | tf_op | source)
XLA Modules:
  0.0 91.0 jit_solution(12480803973728604844)
XLA Ops:
  1.9 0.0 copy-start.1
  1.9 0.6 copy-done.1
  2.6 0.7 copy.8.scales
  3.3 85.7 %shard_map.77 = (f32[32,256]{1,0:T(8,128)}, f32[32,256]{1,0:T(8,128)}) custom-call(f32[16,256]{1,0:T(8,128)} %points.1, f32[16,1]{1,0:T(8,128)} %copy.8.scales, f32[1]{0:T(128)S(6)} %copy.11.signal, f32[1]{0:T(128)S(6)} %copy.12.noise, f32[1,256]{1,0:T(1,128)} %bitcast.2, s32[31,256]{1,0:T(8,128)} %bits.1), custom_call_target="tpu_custom_call" | custom-call | tf_op jit(solution)/shard_map/pallas_call | solution.py:302
  89.0 0.0 copy-start
  89.0 1.4 %copy.13 = f32[32,256]{1,0:T(8,128)} copy(f32[32,256]{1,0:T(8,128)} %get-tuple-element.4) | data formatting | bytes 65536
  90.4 0.0 copy-done
  90.4 0.6 copy.14
Async XLA Ops:
  1.9 0.7 copy-start.1
  89.0 1.4 %copy-start = (f32[32,256]{1,0:T(8,128)S(1)}, f32[32,256]{1,0:T(8,128)}, u32[]{:S(2)}) copy-start(f32[32,256]{1,0:T(8,128)} %get-tuple-element.5) | copy-start | bytes 98308
